TPU v7x, 256 devices: a whole 4x4x8 slice. The times are simulated.
256 devices in a mesh: dp: 16 (over x, y_hi, core), tensor: 16 (over y_lo, z).
Axes of the slice: x: 4, y: 4 (y_hi: 2, y_lo: 2; y = y_hi * 2 + y_lo), z: 8, core: 2. Of those that a mesh axis runs over, the one named last changes fastest.
Arguments:
- enc_hidden: bfloat16 [32768, 4096], P(('dp', 'tensor')), parts along dimension 0, may hold values from -6 to 6
- enc_gain: float32 [4096], replicated, may hold values from 0.1 to 1.9
- dec_hidden: bfloat16 [8192, 4096], P(('dp', 'tensor')), parts along dimension 0, may hold values from -6 to 6
- dec_gain: float32 [4096], replicated, may hold values from 0.8 to 12, as said below
- w_query: bfloat16 [4096, 4096], P(None, 'tensor'), may hold values from -0.046875 to 0.046875
- w_key: bfloat16 [4096, 4096], P(None, 'tensor'), may hold values from -0.09375 to 0.09375
- w_value: bfloat16 [4096, 4096], P(None, 'tensor'), may hold values from -0.09375 to 0.09375
- w_out: bfloat16 [4096, 4096], P('tensor'), may hold values from -0.75 to 0.75
- enc_length: int32 [16], P('dp'), parts along dimension 0, may hold values from 1024 to 2048
- dec_length: int32 [16], P('dp'), parts along dimension 0, may hold values from 256 to 512
Outputs:
- memory: bfloat16 [32768, 4096], P(('dp', 'tensor')), parts along dimension 0
- cross_out: bfloat16 [8192, 4096], P(('dp', 'tensor')), parts along dimension 0
There are 16 independent parts, one for each index of `dp`. A program takes and returns all parts, laid end to end along the dimension named above; an argument that names none is the same for every part. Nothing has to cross between parts.
Inputs may be any that keep to these rules, and one draw needn't show every extreme that they name: `dec_gain`: positive.
All inputs are finite; a program needn't handle non-finite values.
Results may differ from a plain program's by a relative error of at most 0.02.
The roundings to bfloat16 on the way count: a program that leaves them out, or rounds other values in their place, can miss the bound.
Values may be sent and summed in bfloat16 or wider, within the bound.
A program may use at most 128 MiB of HBM per device.

v0:
```python
import jax
import jax.numpy as jnp
from jax import lax
from jax.sharding import Mesh
from jax.sharding import PartitionSpec as P

HEAD_DIM = 64
ENC_LEN = 2048
DEC_LEN = 512
TENSOR = ("tensor_0", "tensor_1")
DP_TENSOR = ("dp", "tensor_0", "tensor_1")


def in_order(parts, dim):
    parts = jnp.moveaxis(parts, 0, dim)
    lengths = parts.shape
    return parts.reshape(*lengths[:dim], lengths[dim] * lengths[dim + 1], *lengths[dim + 2 :])


def all_blocks(array, axes, sequence):
    parts = array
    for k in sequence:
        parts = lax.all_gather(parts, axes[k])
    done = sequence[::-1]
    back = [done.index(k) for k in range(len(axes))]
    parts = parts.transpose(*back, *range(len(axes), parts.ndim))
    return parts.reshape(-1, *array.shape)


def gather_axes(array, axes, sequence, dim):
    return in_order(all_blocks(array, axes, sequence), dim)


def own_block(parts, axes, sequence):
    lengths = [lax.axis_size(a) for a in axes]
    parts = parts.reshape(*lengths, *parts.shape[1:])
    parts = parts.transpose(*sequence, *range(len(axes), parts.ndim))
    parts = parts.reshape(-1, *parts.shape[len(axes) :])
    for k in sequence:
        parts = lax.psum_scatter(parts, axes[k], scatter_dimension=0, tiled=True)
    return parts[0]


def split_up(array, dim, size):
    before, after = (array.shape[:dim], array.shape[dim + 1 :])
    return jnp.moveaxis(array.reshape(*before, size, -1, *after), dim, 0)


def sum_by_axis_2(array, axes, sequence, dim):
    size = lax.axis_size(axes)
    return own_block(split_up(array, dim, size), axes, sequence)


def rms_norm(values, gain):
    wide = values.astype(jnp.float32)
    mean_sq = jnp.mean(wide * wide, axis=-1, keepdims=True)
    return (wide * lax.rsqrt(mean_sq + 1e-06) * gain).astype(jnp.bfloat16)


def shards(
    enc_hidden,
    enc_gain,
    dec_hidden,
    dec_gain,
    w_query,
    w_key,
    w_value,
    w_out,
    enc_length,
    dec_length,
):
    memory = rms_norm(enc_hidden, enc_gain)
    normed = rms_norm(dec_hidden, dec_gain)
    local_width = w_query.shape[1]
    local_heads = local_width // HEAD_DIM
    dec_rows = dec_hidden.shape[0]
    all_normed = gather_axes(normed, TENSOR, (0, 1), 0)
    queries = jnp.dot(all_normed, w_query, preferred_element_type=jnp.float32).astype(jnp.bfloat16)
    q_heads = queries.reshape(DEC_LEN, local_heads, HEAD_DIM)
    segment = lax.all_gather(memory, TENSOR, axis=0, tiled=True)
    key_part = jnp.dot(segment, w_key, preferred_element_type=jnp.float32).astype(jnp.bfloat16)
    value_part = jnp.dot(segment, w_value, preferred_element_type=jnp.float32).astype(jnp.bfloat16)
    paired = jnp.concatenate([key_part, value_part], axis=1)
    key_rows = paired[:, :local_width]
    value_rows = paired[:, local_width:]
    k_heads = key_rows.reshape(ENC_LEN, local_heads, HEAD_DIM)
    scores = jnp.einsum("qhd,khd->hqk", q_heads, k_heads, preferred_element_type=jnp.float32)
    valid_keys = jnp.arange(ENC_LEN, dtype=jnp.int32) < enc_length[0]
    scores = jnp.where(valid_keys[None, None, :], scores, -jnp.inf)
    weights = jax.nn.softmax(scores, axis=-1).astype(jnp.bfloat16)
    v_heads = value_rows.reshape(ENC_LEN, local_heads, HEAD_DIM)
    context = jnp.einsum("hqk,khd->qhd", weights, v_heads, preferred_element_type=jnp.float32)
    context = context.astype(jnp.bfloat16).reshape(DEC_LEN, local_width)
    projected = sum_by_axis_2(
        jnp.dot(context, w_out, preferred_element_type=jnp.float32).astype(jnp.bfloat16),
        TENSOR,
        (1, 0),
        0,
    ).astype(jnp.float32)
    row_ids = lax.axis_index(TENSOR) * dec_rows + jnp.arange(dec_rows, dtype=jnp.int32)
    live_rows = row_ids < dec_length[0]
    cross_out = jnp.where(live_rows[:, None], projected, 0.0).astype(jnp.bfloat16)
    return (memory, cross_out)


def solution(mesh):
    torus = Mesh(mesh.devices.reshape(mesh.shape["dp"], 2, 8), ("dp", "tensor_0", "tensor_1"))
    in_specs = (
        P(DP_TENSOR, None),
        P(),
        P(DP_TENSOR, None),
        P(),
        P(None, TENSOR),
        P(None, TENSOR),
        P(None, TENSOR),
        P(TENSOR, None),
        P("dp"),
        P("dp"),
    )
    out_specs = (P(DP_TENSOR, None), P(DP_TENSOR, None))
    return jax.shard_map(
        shards, mesh=torus, in_specs=in_specs, out_specs=out_specs, check_vma=False
    )
```

profile of v0, /device:TPU:8, one launch (start us, length us, event | category | flops | bytes accessed | tf_op | source)
XLA Modules:
  0.0 385.7 jit_solution(12734843843932825123)
XLA Ops:
  7.2 0.0 copy-start
  7.2 0.0 all-gather.7.cloned.1.call-start
  7.2 1.2 fusion.11
  8.5 1.1 fusion.13
  9.6 8.8 %all-gather = bf16[64,4096]{1,0:T(8,128)(2,1)} all-gather(bf16[32,4096]{1,0:T(8,128)(2,1)S(1)} %fusion.13), channel_id=2, replica_groups=mesh['dp'=16,'tensor_0'=2,'tensor_1'=8] {'tensor_0'}, dimensions={0}, use_global_device_ids=true | all-gather | bytes 786432 | tf_op jit(solution)/shard_map/all_gather | solution.py:23
  18.4 0.0 all-gather.7.cloned.1.call-update
  18.4 0.0 all-gather.5.cloned.1.call-start
  18.5 1.5 fusion.7
  20.0 2.5 fusion.9
  22.5 0.0 all-gather.5.cloned.1.call-update
  22.6 0.0 reduce-scatter.3.cloned.1.call-start
  23.3 52.9 %all-gather.7.cloned.1.call-done = bf16[16,32,4096]{2,1,0:T(8,128)(2,1)} async-done(((bf16[2,32,4096]{2,1,0:T(8,128)(2,1)}), bf16[16,32,4096]{2,1,0:T(8,128)(2,1)}) %all-gather.7.cloned.1.call-update) | async-done | bytes 4194320 | tf_op jit(solution)/shard_map/all_gather | solution.py:23
  76.2 0.0 copy-start.1
  76.2 2.6 copy.16
  78.8 0.2 copy-done.1
  79.1 1.3 convolution_convert_fusion.3
  80.4 181.1 %all-gather.5.cloned.1.call-done = bf16[2048,4096]{1,0:T(8,128)(2,1)} async-done(((bf16[128,4096]{1,0:T(8,128)(2,1)}), bf16[2048,4096]{1,0:T(8,128)(2,1)}) %all-gather.5.cloned.1.call-update) | async-done | bytes 16777232 | tf_op jit(solution)/shard_map/all_gather | solution.py:80
  261.5 10.9 %convolution_convert_fusion.1 = bf16[2048,256]{0,1:T(8,128)(2,1)S(1)} fusion(bf16[2048,4096]{1,0:T(8,128)(2,1)} %all-gather.5.cloned.1.call-done, bf16[4096,256]{1,0:T(8,128)(2,1)} %param.15), kind=kOutput, calls=%fused_computation.11 | convolution fusion | flops 4295491584 | bytes 19922944 | tf_op jit(solution)/shard_map/dot_general | solution.py:81
  272.4 8.5 %fusion.18 = (f32[4,512]{1,0:T(4,128)S(1)}, f32[4,512,2048]{2,1,0:T(8,128)}) fusion(pred[2048]{0:T(1024)(128)(4,1)S(1)} %iota_compare_fusion, bf16[512,4,64]{0,2,1:T(8,128)(2,1)S(1)} %bitcast.43, bf16[2048,4,64]{0,2,1:T(8,128)(2,1)S(1)} %bitcast.41), kind=kOutput, calls=%fused_computation.31 | convolution fusion | flops 549455872 | bytes 18098176 | tf_op jit(solution)/shard_map/sub | solution.py:90
  280.8 10.9 %convolution_convert_fusion.2 = bf16[2048,256]{0,1:T(8,128)(2,1)S(1)} fusion(bf16[2048,4096]{1,0:T(8,128)(2,1)} %all-gather.5.cloned.1.call-done, bf16[4096,256]{1,0:T(8,128)(2,1)} %param.16), kind=kOutput, calls=%fused_computation.12 | convolution fusion | flops 4295491584 | bytes 19922944 | tf_op jit(solution)/shard_map/dot_general | solution.py:82
  291.7 8.5 %fusion.10 = bf16[4,64,512]{2,1,0:T(8,128)(2,1)S(1)} fusion(bf16[2048,4,64]{0,2,1:T(8,128)(2,1)S(1)} %bitcast.42, f32[4,512,2048]{2,1,0:T(8,128)} %get-tuple-element.3, f32[4,512]{1,0:T(4,128)S(1)} %get-tuple-element.2), kind=kOutput, calls=%fused_computation.17 | convolution fusion | flops 545390592 | bytes 18096128 | tf_op jit(solution)/shard_map/hqk,khd->qhd/dot_general | solution.py:92
  300.2 0.0 copy-done
  300.2 1.3 convolution_convert_fusion
  301.5 2.2 copy.17
  303.7 0.0 reduce-scatter.3.cloned.1.call-update
  303.7 0.0 reduce-scatter.5.cloned.1.call-start
  303.8 54.1 %reduce-scatter.3.cloned.1.call-done = bf16[2,32,4096]{2,1,0:T(8,128)(2,1)} async-done(((bf16[16,32,4096]{2,1,0:T(8,128)(2,1)}), bf16[2,32,4096]{2,1,0:T(8,128)(2,1)}) %reduce-scatter.3.cloned.1.call-update) | async-done | bytes 524304 | tf_op jit(solution)/shard_map/reduce_scatter | solution.py:40
  357.9 0.0 reduce-scatter.5.cloned.1.call-update
  358.6 18.9 %reduce-scatter.5.cloned.1.call-done = bf16[1,32,4096]{2,1,0:T(8,128)(2,1)} async-done(((bf16[2,32,4096]{2,1,0:T(8,128)(2,1)}), bf16[1,32,4096]{2,1,0:T(8,128)(2,1)}) %reduce-scatter.5.cloned.1.call-update) | async-done | bytes 262160 | tf_op jit(solution)/shard_map/reduce_scatter | solution.py:40
  377.4 1.8 fusion.14
  (4 shorter events, 0.0 us)
Async XLA Ops:
  7.2 293.1 %copy-start = (bf16[256,4096]{1,0:T(8,128)(2,1)S(1)}, bf16[256,4096]{1,0:T(8,128)(2,1)}, u32[]{:S(2)}) copy-start(bf16[256,4096]{1,0:T(8,128)(2,1)} %param.17) | copy-start | bytes 6291460
  7.2 69.0 %all-gather.7.cloned.1.call-start = ((), (), s32[]{:S(2)}) async-start(), calls=%async_computation.5 | async-start | bytes 4718592 | tf_op jit(solution)/shard_map/all_gather | solution.py:23
  18.4 243.0 %all-gather.5.cloned.1.call-start = ((), (), s32[]{:S(2)}) async-start(), calls=%async_computation.2 | async-start | bytes 17825792 | tf_op jit(solution)/shard_map/all_gather | solution.py:80
  22.6 335.3 %reduce-scatter.3.cloned.1.call-start = ((), (), s32[]{:S(2)}) async-start(), calls=%async_computation.3 | async-start | bytes 4718592 | tf_op jit(solution)/shard_map/reduce_scatter | solution.py:40
  76.2 2.9 copy-start.1
  303.7 73.7 %reduce-scatter.5.cloned.1.call-start = ((), (), s32[]{:S(2)}) async-start(), calls=%async_computation.4 | async-start | bytes 786432 | tf_op jit(solution)/shard_map/reduce_scatter | solution.py:40
Sparse Core Ops, SparseCore 0:
  18.5 57.6 all-gather.6
  78.6 182.8 all-gather.4
  303.9 53.9 reduce-scatter.2
  360.2 17.1 reduce-scatter.4
where the time goes:
time: 388 us; the launch traced here: 386 us
  waiting for transfers between devices  307 us (79%)
  matrix products  41.3 us (11%)
  between operations  15.1 us (4%)
  blocking collectives  8.82 us (2%)
  other arithmetic  8.18 us (2%)
  local copies, waits for them, and re-layouts  5.06 us (1%)
    all_gather x1, waiting for transfers between devices, shards(): segment = lax.all_gather(memory, TENSOR, axis=0, tiled=True)  181 us
    reduce_scatter x2, waiting for transfers between devices, own_block(): parts = lax.psum_scatter(parts, axes[k], scatter_dimension=0, tiled=True)  73 us
    all_gather x1, waiting for transfers between devices, all_blocks(): parts = lax.all_gather(parts, axes[k])  52.9 us
    dot_general x1, matrix products, shards(): jnp.dot(segment, w_key, preferred_element_type=jnp.float32)  10.9 us
    dot_general x1, matrix products, shards(): jnp.dot(segment, w_value, preferred_element_type=jnp.float32)  10.9 us
    all_gather x1, blocking collectives, all_blocks(): parts = lax.all_gather(parts, axes[k])  8.82 us
    dot_general x1, matrix products, shards(): jnp.einsum('hqk,khd->qhd', weights, v_heads, preferred_element_type=jnp.f...  8.49 us
    sub x1, matrix products, shards(): weights = jax.nn.softmax(scores, axis=-1).astype(jnp.bfloat16)  8.48 us
  transfers between devices with their start and end apart: 4, of which 4 were waited for; matrix products, arithmetic and copies ran while one was open for 2% of the time, Pallas kernels for 0%

commit v1 on v0

v1 whole, which is shorter than its diff:
```python
import functools

import jax
import jax.numpy as jnp
from jax import lax
from jax.experimental import pallas as pl
from jax.experimental.pallas import tpu as pltpu
from jax.sharding import Mesh
from jax.sharding import PartitionSpec as P

HEAD_DIM = 64
MESH = pl.DeviceIdType.MESH
NZ = 8
NEG = -1e30
ROWS = ("x", "yh", "c", "yl", "z")
BF16, F32 = jnp.bfloat16, jnp.float32

R_ITEMS = (
    [("n", 0, 0), ("m", 0, 0), ("n", 1, 0), ("m", 0, 1), ("n", 2, 0), ("m", 0, 2), ("n", 3, 0), ("m", 0, 3)]
    + [("m", 1, p) for p in range(4)]
    + [("m", 2, p) for p in range(4)]
    + [("m", 3, 0)]
)
L_ITEMS = (
    [("n", 0, 0), ("m", 0, 0), ("n", 1, 0), ("m", 0, 1), ("n", 2, 0), ("m", 0, 2), ("m", 0, 3)]
    + [("m", 1, p) for p in range(4)]
    + [("m", 2, p) for p in range(4)]
    + [("m", 3, p) for p in (1, 2, 3)]
)


def schedule(items):
    after, last = {}, -1
    for i, (kind, hop, piece) in enumerate(items):
        need = items.index((kind, hop - 1, piece)) if hop else -1
        last = max(last, need)
        after.setdefault(last, []).append(i)
    return after


def kernel(
    len_ref, n_hbm, m_hbm, wq_hbm, wk_hbm, wv_hbm, wo_hbm, out_ref,
    gn, gm, w, wo, kv, q, qtm, vt, acc, mx, sm, ctx, prod, rs_send, rs_recv,
    loc, z_send, z_recv, wy_send, wy_recv, xa_send, xa_recv, xb_send, xb_recv, c_send, c_recv,
    q_sem, kv_send, kv_recv, rss, rsr,
):
    x, c = lax.axis_index("x"), lax.axis_index("c")
    y, z = lax.axis_index("yl"), lax.axis_index("z")
    yn, cn = 1 - y, 1 - c
    xa, xb = x + 1 - 2 * (x % 2), 3 - x
    right, left = (z + 1) % NZ, (z + NZ - 1) % NZ
    peers = ({"z": right}, {"z": left}, {"yl": yn}, {"x": xa}, {"x": xb}, {"c": cn})

    barrier = pltpu.get_barrier_semaphore()
    for peer in peers:
        pl.semaphore_signal(barrier, inc=1, device_id=peer, device_id_type=MESH)
    pl.semaphore_wait(barrier, len(peers))

    def remote(src, dst, ssem, rsem, peer):
        return pltpu.make_async_remote_copy(
            src_ref=src, dst_ref=dst, send_sem=ssem, recv_sem=rsem, device_id=peer, device_id_type=MESH
        )

    def z_ref(kind, owner, piece):
        return gn.at[owner] if kind == "n" else gm.at[owner, pl.ds(32 * piece, 32), :]

    def z_copy(d, i, receive):
        kind, hop, piece = (R_ITEMS, L_ITEMS)[d][i]
        shift = hop + (1 if receive else 0)
        owner = (z + (NZ - shift if d == 0 else shift)) % NZ
        dst = z_ref(kind, owner, piece)
        src = dst
        if hop == 0 and not receive:
            src = n_hbm if kind == "n" else m_hbm.at[pl.ds(32 * piece, 32), :]
        return remote(src, dst, z_send.at[d, i], z_recv.at[d, i], peers[d])

    plan = (schedule(R_ITEMS), schedule(L_ITEMS))

    def z_issue(d, k):
        for i in plan[d].get(k, ()):
            z_copy(d, i, False).start()

    def serve(d, k):
        z_copy(d, k, True).wait_recv()
        z_issue(d, k)

    hbm = (wk_hbm, wv_hbm, wq_hbm, wo_hbm)
    STEP = (512, 512, 512, 32)

    def part(t, e, n=1):
        rows = pl.ds(e * STEP[t], n * STEP[t])
        return wo.at[1, rows, :] if t == 3 else w.at[1, t, rows, :]

    mine = c * 4 + x

    def wy(t):
        src = hbm[t].at[pl.ds(mine * STEP[t], STEP[t]), :]
        return remote(src, part(t, mine), wy_send.at[t], wy_recv.at[t], peers[2])

    def wxa(t, receive=False):
        r = part(t, c * 4 + (xa if receive else x))
        return remote(r, r, xa_send.at[t], xa_recv.at[t], peers[3])

    def wxb(t, k, receive=False):
        near, far = (xb, xb + 1 - 2 * (xb % 2)) if receive else (x, xa)
        r = part(t, c * 4 + (far if k else near))
        return remote(r, r, xb_send.at[t, k], xb_recv.at[t, k], peers[4])

    def wc(t, receive=False):
        r = part(t, 4 * (cn if receive else c), 4)
        return remote(r, r, c_send.at[t], c_recv.at[t], peers[5])

    def got_y(t):
        wy(t).wait_recv()
        wxb(t, 0).start()
        wxa(t).start()

    def got_xa(t):
        wxa(t, True).wait_recv()
        wxb(t, 1).start()

    def got_xb(t):
        wxb(t, 0, True).wait_recv()
        wxb(t, 1, True).wait_recv()
        wc(t).start()

    for d in (0, 1):
        z_issue(d, -1)
    for t in range(4):
        wy(t).start()
    local = [
        pltpu.make_async_copy(n_hbm, gn.at[z], loc.at[0]),
        pltpu.make_async_copy(m_hbm, gm.at[z], loc.at[1]),
        pltpu.make_async_copy(wk_hbm, w.at[0, 0], loc.at[2]),
        pltpu.make_async_copy(wv_hbm, w.at[0, 1], loc.at[3]),
        pltpu.make_async_copy(wq_hbm, w.at[0, 2], loc.at[4]),
        pltpu.make_async_copy(wo_hbm, wo.at[0], loc.at[5]),
    ]
    for copy in local:
        copy.start()
    mx[...] = jnp.full_like(mx, NEG)
    sm[...] = jnp.zeros_like(sm)
    acc[...] = jnp.zeros_like(acc)

    def both(k):
        serve(0, k)
        serve(1, k)

    both(0)
    got_y(0)
    got_y(1)
    got_xa(0)
    both(1)
    got_y(2)
    got_xa(1)
    both(2)
    got_y(3)
    got_xa(2)
    got_xb(0)
    both(3)
    got_xb(1)
    got_xa(3)
    both(4)
    both(5)
    got_xb(2)
    both(6)
    serve(0, 7)
    for copy in local:
        copy.wait()
    for t in (2, 0, 1):
        wc(t, True).wait_recv()

    q_copy = remote(q.at[2], q.at[1], q_sem.at[0], q_sem.at[1], peers[2])
    tokens = gn[...].reshape(NZ * 32, gn.shape[2])

    @pl.loop(0, 2)
    def _(i):
        q[2 - 2 * i] = jnp.dot(tokens, w[1 - i, 2], preferred_element_type=F32).astype(BF16)

    q_copy.start()

    def block_of(j):
        near = (j + 1) // 2
        return (z + NZ + near - 2 * near * (j % 2)) % NZ

    def kv_copy(j):
        zb = block_of(j)
        return remote(kv.at[2, zb], kv.at[1, zb], kv_send.at[j], kv_recv.at[j], peers[2])

    def project(j):
        zb = block_of(j)
        rows = gm[zb]

        @pl.loop(0, 4)
        def _(i):
            own, which = i // 2, i % 2
            kv[2 - 2 * own, zb, which] = jnp.dot(
                rows, w[1 - own, which], preferred_element_type=F32
            ).astype(BF16)

        kv_copy(j).start()

    def attend(j):
        zb = block_of(j)
        kv_copy(j).wait_recv()
        keys = jnp.concatenate([kv[0, zb, 0], kv[1, zb, 0]], axis=0)
        values = jnp.concatenate([kv[0, zb, 1], kv[1, zb, 1]], axis=0)
        vt[...] = values.T
        length = len_ref[0]
        row = lax.broadcasted_iota(jnp.int32, (128, 1), 0)
        index = jnp.concatenate([row + (y * NZ + zb) * 128, row + (yn * NZ + zb) * 128], axis=0)
        valid = jnp.broadcast_to(index, (256, 256)) < length

        @pl.loop(0, 4)
        def _(h):
            v_h = vt[pl.ds(pl.multiple_of(h * 64, 64), 64), :]
            for half in range(2):
                cols = pl.ds(half * 256, 256)
                s = jnp.dot(keys, qtm[h, :, cols], preferred_element_type=F32)
                s = jnp.where(valid, s, NEG)
                old = mx[h, :, cols]
                new = jnp.maximum(old, jnp.max(s, axis=0, keepdims=True))
                p = jnp.exp(s - new)
                scale = jnp.exp(old - new)
                mx[h, :, cols] = new
                sm[h, :, cols] = scale * sm[h, :, cols] + jnp.sum(p, axis=0, keepdims=True)
                acc[h, :, cols] = scale * acc[h, :, cols] + jnp.dot(
                    v_h, p.astype(BF16), preferred_element_type=F32
                )

    project(0)
    q_copy.wait_recv()
    first = jnp.where(y == 0, q[0], q[1])
    second = jnp.where(y == 0, q[1], q[0])
    qt = jnp.concatenate([first.T, second.T], axis=1)
    lane = lax.broadcasted_iota(jnp.int32, (256, 512), 0)
    for h in range(4):
        qtm[h] = jnp.where(lane // HEAD_DIM == h, qt, jnp.zeros_like(qt))

    need = {
        1: [(1, 7), (0, 8)],
        2: [(1, 8), (0, 9)],
        3: [(0, 10), (1, 9), (0, 11), (1, 10)],
        5: [(d, k) for i in range(4) for d, k in ((0, 12 + i), (1, 11 + i))],
        7: [(1, 15), (0, 16), (1, 16), (1, 17)],
    }

    @pl.loop(1, NZ)
    def _(j):
        for jj, todo in need.items():

            @pl.when(j == jj)
            def _():
                for d, k in todo:
                    serve(d, k)

        @pl.when(j == 4)
        def _():
            got_xb(3)

        project(j)
        attend(j - 1)

    attend(NZ - 1)
    wc(3, True).wait_recv()

    full = [(acc[h] * (1.0 / sm[h])).astype(BF16) for h in range(4)]
    full = jnp.concatenate(full, axis=0)
    low, high = full[:, :256].T, full[:, 256:].T
    ctx[2] = jnp.where(y == 0, high, low)
    ctx_copy = remote(ctx.at[2], ctx.at[1], q_sem.at[2], q_sem.at[3], peers[2])
    ctx_copy.start()
    ctx[0] = jnp.where(y == 0, low, high)
    ctx_copy.wait_recv()

    @pl.loop(0, 8)
    def _(i):
        cols = pl.ds(pl.multiple_of(i * 512, 512), 512)
        prod[:, cols] = jnp.dot(ctx[0], wo[0, :, cols], preferred_element_type=F32) + jnp.dot(
            ctx[1], wo[1, :, cols], preferred_element_type=F32
        )

    orders = (
        [(0, 4), (1, 3), (0, 3), (1, 2), (0, 2), (1, 1), (0, 1)],
        [(1, 4), (0, 3), (1, 3), (0, 2), (1, 2), (0, 1), (1, 1)],
    )

    def rs_copy(d, i):
        return remote(rs_send.at[d, i], rs_recv.at[d, i], rss.at[d, i], rsr.at[d, i], peers[d])

    def own_rows(owner, half):
        rows = pl.ds(pl.multiple_of(owner * 32, 32), 32)
        return prod[rows, pl.ds(half * 2048, 2048)]

    for i in range(7):
        for d in (0, 1):
            half, far = orders[d][i]
            owner = (z + (far if d == 0 else NZ - far)) % NZ
            term = own_rows(owner, half)
            if i >= 2:
                rs_copy(d, i - 2).wait_recv()
                term = term + rs_recv[d, i - 2].astype(F32)
            rs_send[d, i] = term.astype(BF16)
            rs_copy(d, i).start()
    for d in (0, 1):
        for i in (5, 6):
            rs_copy(d, i).wait_recv()
    for half in (0, 1):
        total = own_rows(z, half)
        total = total + rs_recv[0, 6 - half].astype(F32) + rs_recv[1, 5 + half].astype(F32)
        out_ref[:, pl.ds(half * 2048, 2048)] = total.astype(BF16)

    for d in (0, 1):
        for i in range(len((R_ITEMS, L_ITEMS)[d])):
            z_copy(d, i, False).wait_send()
        for i in range(7):
            rs_copy(d, i).wait_send()
    for t in range(4):
        wy(t).wait_send()
        wxa(t).wait_send()
        wxb(t, 0).wait_send()
        wxb(t, 1).wait_send()
        wc(t).wait_send()
    q_copy.wait_send()
    ctx_copy.wait_send()
    for j in range(NZ):
        kv_copy(j).wait_send()


def rms_norm(values, gain):
    wide = values.astype(F32)
    mean_sq = jnp.mean(wide * wide, axis=-1, keepdims=True)
    return (wide * lax.rsqrt(mean_sq + 1e-06) * gain).astype(BF16)


def shards(enc_hidden, enc_gain, dec_hidden, dec_gain, w_query, w_key, w_value, w_out, enc_length, dec_length):
    memory = rms_norm(enc_hidden, enc_gain)
    normed = rms_norm(dec_hidden, dec_gain)
    width = w_query.shape[0]
    rows = dec_hidden.shape[0]
    anywhere = pl.BlockSpec(memory_space=pl.ANY)
    dma = pltpu.SemaphoreType.DMA
    summed = pl.pallas_call(
        kernel,
        out_shape=jax.ShapeDtypeStruct((rows, width), BF16),
        in_specs=[pl.BlockSpec(memory_space=pltpu.SMEM)] + [anywhere] * 6,
        out_specs=pl.BlockSpec(memory_space=pltpu.VMEM),
        scratch_shapes=[
            pltpu.VMEM((NZ, 32, width), BF16),
            pltpu.VMEM((NZ, 128, width), BF16),
            pltpu.VMEM((2, 3, width, 256), BF16),
            pltpu.VMEM((2, 256, width), BF16),
            pltpu.VMEM((3, NZ, 2, 128, 256), BF16),
            pltpu.VMEM((3, 256, 256), BF16),
            pltpu.VMEM((4, 256, 512), BF16),
            pltpu.VMEM((256, 256), BF16),
            pltpu.VMEM((4, 64, 512), F32),
            pltpu.VMEM((4, 1, 512), F32),
            pltpu.VMEM((4, 1, 512), F32),
            pltpu.VMEM((3, 256, 256), BF16),
            pltpu.VMEM((256, width), F32),
            pltpu.VMEM((2, 7, 32, width // 2), BF16),
            pltpu.VMEM((2, 7, 32, width // 2), BF16),
            dma((6,)),
            dma((2, 18)),
            dma((2, 18)),
            dma((4,)),
            dma((4,)),
            dma((4,)),
            dma((4,)),
            dma((4, 2)),
            dma((4, 2)),
            dma((4,)),
            dma((4,)),
            dma((4,)),
            dma((NZ,)),
            dma((NZ,)),
            dma((2, 7)),
            dma((2, 7)),
        ],
        compiler_params=pltpu.CompilerParams(
            collective_id=0, has_side_effects=True, vmem_limit_bytes=60 * 1024 * 1024
        ),
        name="cross_attention",
    )(enc_length, normed, memory, w_query, w_key, w_value, w_out)
    row_ids = (lax.axis_index("yl") * NZ + lax.axis_index("z")) * rows + jnp.arange(rows, dtype=jnp.int32)
    cross_out = jnp.where((row_ids < dec_length[0])[:, None], summed, jnp.zeros_like(summed))
    return (memory, cross_out)


def solution(mesh):
    torus = Mesh(mesh.devices.reshape(4, 2, 2, 2, NZ), ROWS)
    tensor = ("yl", "z")
    dp = ("x", "yh", "c")
    in_specs = (
        P(ROWS, None),
        P(),
        P(ROWS, None),
        P(),
        P(None, tensor),
        P(None, tensor),
        P(None, tensor),
        P(tensor, None),
        P(dp),
        P(dp),
    )
    out_specs = (P(ROWS, None), P(ROWS, None))
    return jax.shard_map(shards, mesh=torus, in_specs=in_specs, out_specs=out_specs, check_vma=False)
```

time: 388 us -> 159 us (0.41)
  waiting for transfers between devices: 307 us -> 0 us
  Pallas kernels: 0 us -> 150 us
  matrix products: 41.3 us -> 0 us
  between operations: 15.1 us -> 1.98 us
  blocking collectives: 8.82 us -> 0 us
  local copies, waits for them, and re-layouts: 5.06 us -> 0.01 us
    all_gather x2 -> x0, waiting for transfers between devices: 234 us -> none  [the longest x1 181 us: shards(): segment = lax.all_gather(memory, TENSOR, axis=0, tiled=True)]
    pallas_call x0 -> x1, Pallas kernels: none -> 150 us  [shards(): pl.pallas_call(kernel, out_shape=jax.ShapeDtypeStruct((rows, width), BF16...]
    reduce_scatter x2 -> x0, waiting for transfers between devices: 73 us -> none  [own_block(): parts = lax.psum_scatter(parts, axes[k], scatter_dimension=0, tiled=True)]
    dot_general x5 -> x0, matrix products: 32.8 us -> none  [the longest x1 10.9 us: shards(): jnp.dot(segment, w_key, preferred_element_type=jnp.float32)]
    all_gather x1 -> x0, blocking collectives: 8.82 us -> none  [all_blocks(): parts = lax.all_gather(parts, axes[k])]
    sub x1 -> x0, matrix products: 8.48 us -> none  [shards(): weights = jax.nn.softmax(scores, axis=-1).astype(jnp.bfloat16)]
    transpose x2 -> x0, local copies, waits for them, and re-layouts: 4.81 us -> none  [the longest x1 2.61 us: all_blocks(): parts = parts.transpose(*back, *range(len(axes), parts.ndim))]
  transfers between devices with their start and end apart: 4 -> 0, of which waited for: 4 -> 0; matrix products, arithmetic and copies ran while one was open for 2% -> 0% of each run, Pallas kernels for 0% -> 0%
where the time goes in v1:
time: 159 us
  Pallas kernels  150 us (94%)
  other arithmetic  6.86 us (4%)
  between operations  1.98 us (1%)
    pallas_call x1, Pallas kernels, shards(): pl.pallas_call(kernel, out_shape=jax.ShapeDtypeStruct((rows, width), BF16...  150 us
    convert_element_type x2, other arithmetic, rms_norm(): return (wide * lax.rsqrt(mean_sq + 1e-06) * gain).astype(BF16)  3.36 us

profile of v1, /device:TPU:8, one launch (start us, length us, event | category | flops | bytes accessed | tf_op | source)
XLA Modules:
  0.0 158.7 jit_solution(16918399104399527461)
XLA Ops:
  0.6 0.0 copy-start
  0.6 0.0 copy-start.1
  0.6 1.6 fusion
  2.2 2.5 %fusion.2.m_hbm = bf16[128,4096]{1,0:T(8,128)(2,1)} fusion(bf16[128,4096]{1,0:T(8,128)(2,1)} %param.10, f32[4096]{0:T(1024)} %param.11, f32[128]{0:T(128)S(1)} %add_rsqrt_fusion.1), kind=kLoop, calls=%fused_computation.4 | loop fusion | flops 2097152 | bytes 2114048 | tf_op jit(solution)/shard_map/convert_element_type | solution.py:333
  5.4 0.0 copy-done
  5.4 0.2 fusion.3
  5.6 0.0 copy-done.1
  5.6 0.8 fusion.5.n_hbm
  6.4 149.8 %cross_attention.1 = bf16[32,4096]{1,0:T(8,128)(2,1)} custom-call(s32[1]{0:T(128)S(6)} %copy.12.len_ref, bf16[32,4096]{1,0:T(8,128)(2,1)} %fusion.5.n_hbm, bf16[128,4096]{1,0:T(8,128)(2,1)} %fusion.2.m_hbm, bf16[4096,256]{1,0:T(8,128)(2,1)} %wq_hbm.1, bf16[4096,256]{1,0:T(8,128)(2,1)} %wk_hbm.1, bf16[4096,256]{1,0:T(8,128)(2,1)} %wv_hbm.1, ...), custom_call_target="tpu_custom_call" | custom-call | tf_op jit(solution)/shard_map/cross_attention/pallas_call | solution.py:343
  156.9 1.7 %broadcast_select_fusion = bf16[32,4096]{1,0:T(8,128)(2,1)} fusion(bf16[32,4096]{1,0:T(8,128)(2,1)} %cross_attention.1, pred[32]{0:T(512)(128)(4,1)S(1)} %add_compare_fusion), kind=kLoop, calls=%fused_computation.10 | loop fusion | flops 131072 | bytes 524320 | tf_op jit(solution)/shard_map/jit(_where)/select_n | solution.py:387
  (3 shorter events, 0.0 us)
Async XLA Ops:
  0.6 4.8 %copy-start = (bf16[32,4096]{1,0:T(8,128)(2,1)S(1)}, bf16[32,4096]{1,0:T(8,128)(2,1)}, u32[]{:S(2)}) copy-start(bf16[32,4096]{1,0:T(8,128)(2,1)} %param.12) | copy-start | bytes 786436
  0.6 5.0 %copy-start.1 = (f32[4096]{0:T(1024)S(1)}, f32[4096]{0:T(1024)}, u32[]{:S(2)}) copy-start(f32[4096]{0:T(1024)} %param.13) | copy-start | bytes 49156

commit v2 on v1

v2 whole, which is shorter than its diff:
```python
import functools

import jax
import jax.numpy as jnp
from jax import lax
from jax.experimental import pallas as pl
from jax.experimental.pallas import tpu as pltpu
from jax.sharding import Mesh
from jax.sharding import PartitionSpec as P

HEAD_DIM = 64
MESH = pl.DeviceIdType.MESH
NZ = 8
NEG = -1e30
ROWS = ("x", "yh", "c", "yl", "z")
BF16, F32 = jnp.bfloat16, jnp.float32

R_ITEMS = (
    [("n", 0, 0), ("m", 0, 0), ("n", 1, 0), ("m", 0, 1), ("n", 2, 0), ("m", 0, 2), ("n", 3, 0), ("m", 0, 3)]
    + [("m", 1, p) for p in range(4)]
    + [("m", 2, p) for p in range(4)]
    + [("m", 3, p) for p in (0, 4)]
)
L_ITEMS = (
    [("n", 0, 0), ("m", 0, 0), ("n", 1, 0), ("m", 0, 1), ("n", 2, 0), ("m", 0, 2), ("m", 0, 3)]
    + [("m", 1, p) for p in range(4)]
    + [("m", 2, p) for p in range(4)]
    + [("m", 3, p) for p in (2, 3, 5)]
)


def schedule(items):
    after, last = {}, -1
    for i, (kind, hop, piece) in enumerate(items):
        need = items.index((kind, hop - 1, 1 if piece > 3 else piece)) if hop else -1
        last = max(last, need)
        after.setdefault(last, []).append(i)
    return after


def piece_rows(piece):
    return pl.ds(32 * piece, 32) if piece < 4 else pl.ds(32 + 16 * (piece - 4), 16)


def rms_norm(values, gain):
    wide = values.astype(F32)
    mean_sq = jnp.mean(wide * wide, axis=-1, keepdims=True)
    return (wide * lax.rsqrt(mean_sq + 1e-06) * gain).astype(BF16)


def kernel(
    enc_len_hbm, dec_len_hbm, enc_hbm, encg_hbm, dec_hbm, decg_hbm, wq_hbm, wk_hbm, wv_hbm, wo_hbm, mem_out, out_ref,
    enc_len, dec_len, raw, gain, gn, gm, w, wo, kva, kvb, q, qtm, acc, mx, sm, ctx, both_ctx, rs_send, rs_recv,
    loc, z_send, z_recv, wy_send, wy_recv, xa_send, xa_recv, xb_send, xb_recv, c_send, c_recv,
    q_sem, ctx_sem, kva_send, kva_recv, kvb_send, kvb_recv, rss, rsr,
):
    x, c = lax.axis_index("x"), lax.axis_index("c")
    y, z = lax.axis_index("yl"), lax.axis_index("z")
    yn, cn = 1 - y, 1 - c
    xa, xb = x + 1 - 2 * (x % 2), 3 - x
    right, left = (z + 1) % NZ, (z + NZ - 1) % NZ
    peers = ({"z": right}, {"z": left}, {"yl": yn}, {"x": xa}, {"x": xb}, {"c": cn})

    barrier = pltpu.get_barrier_semaphore()
    for peer in peers:
        pl.semaphore_signal(barrier, inc=1, device_id=peer, device_id_type=MESH)

    enters = [
        pltpu.make_async_copy(dec_hbm, raw.at[pl.ds(0, 32), :], loc.at[0]),
        pltpu.make_async_copy(decg_hbm, gain.at[0], loc.at[1]),
        pltpu.make_async_copy(enc_hbm, raw.at[pl.ds(32, 128), :], loc.at[2]),
        pltpu.make_async_copy(encg_hbm, gain.at[1], loc.at[3]),
    ]
    local = [
        pltpu.make_async_copy(wk_hbm, w.at[0, 0], loc.at[4]),
        pltpu.make_async_copy(wv_hbm, w.at[0, 1], loc.at[5]),
        pltpu.make_async_copy(wq_hbm, w.at[0, 2], loc.at[6]),
        pltpu.make_async_copy(wo_hbm, wo.at[0], loc.at[7]),
        pltpu.make_async_copy(enc_len_hbm, enc_len, loc.at[9]),
        pltpu.make_async_copy(dec_len_hbm, dec_len, loc.at[10]),
    ]
    for copy in enters + local:
        copy.start()
    enters[0].wait()
    enters[1].wait()
    gn[z] = rms_norm(raw[pl.ds(0, 32), :], gain[0])
    enters[2].wait()
    enters[3].wait()

    def norm_piece(p):
        gm[z, pl.ds(32 * p, 32), :] = rms_norm(raw[pl.ds(32 + 32 * p, 32), :], gain[1])

    norm_piece(0)
    pl.semaphore_wait(barrier, len(peers))

    def remote(src, dst, ssem, rsem, peer):
        return pltpu.make_async_remote_copy(
            src_ref=src, dst_ref=dst, send_sem=ssem, recv_sem=rsem, device_id=peer, device_id_type=MESH
        )

    def z_ref(kind, owner, piece):
        return gn.at[owner] if kind == "n" else gm.at[owner, piece_rows(piece), :]

    def z_copy(d, i, receive):
        kind, hop, piece = (R_ITEMS, L_ITEMS)[d][i]
        shift = hop + (1 if receive else 0)
        owner = (z + (NZ - shift if d == 0 else shift)) % NZ
        block = z_ref(kind, owner, piece)
        return remote(block, block, z_send.at[d, i], z_recv.at[d, i], peers[d])

    plan = (schedule(R_ITEMS), schedule(L_ITEMS))

    def z_issue(d, k):
        for i in plan[d].get(k, ()):
            z_copy(d, i, False).start()

    def serve(d, k):
        z_copy(d, k, True).wait_recv()
        z_issue(d, k)

    hbm = (wk_hbm, wv_hbm, wq_hbm, wo_hbm)
    STEP = (512, 512, 512, 32)

    def part(t, e, n=1):
        rows = pl.ds(e * STEP[t], n * STEP[t])
        return wo.at[1, rows, :] if t == 3 else w.at[1, t, rows, :]

    mine = c * 4 + x

    def wy(t):
        src = hbm[t].at[pl.ds(mine * STEP[t], STEP[t]), :]
        return remote(src, part(t, mine), wy_send.at[t], wy_recv.at[t], peers[2])

    def wxa(t, receive=False):
        r = part(t, c * 4 + (xa if receive else x))
        return remote(r, r, xa_send.at[t], xa_recv.at[t], peers[3])

    def wxb(t, k, receive=False):
        near, far = (xb, xb + 1 - 2 * (xb % 2)) if receive else (x, xa)
        r = part(t, c * 4 + (far if k else near))
        return remote(r, r, xb_send.at[t, k], xb_recv.at[t, k], peers[4])

    def wc(t, receive=False):
        r = part(t, 4 * (cn if receive else c), 4)
        return remote(r, r, c_send.at[t], c_recv.at[t], peers[5])

    def got_y(t):
        wy(t).wait_recv()
        wxb(t, 0).start()
        wxa(t).start()

    def got_xa(t):
        wxa(t, True).wait_recv()
        wxb(t, 1).start()

    def got_xb(t):
        wxb(t, 0, True).wait_recv()
        wxb(t, 1, True).wait_recv()
        wc(t).start()

    for d in (0, 1):
        z_issue(d, -1)
    for t in range(4):
        wy(t).start()
    @pl.loop(1, 4)
    def _(p):
        norm_piece(p)

    mem_out[...] = gm[z]
    mx[...] = jnp.full_like(mx, NEG)
    sm[...] = jnp.zeros_like(sm)
    acc[...] = jnp.zeros_like(acc)

    def both(k):
        serve(0, k)
        serve(1, k)

    both(0)
    got_y(0)
    got_y(1)
    got_xa(0)
    both(1)
    got_y(2)
    got_xa(1)
    both(2)
    got_y(3)
    got_xa(2)
    got_xb(0)
    both(3)
    got_xb(1)
    got_xa(3)
    both(4)
    both(5)
    got_xb(2)
    both(6)
    serve(0, 7)
    for copy in local:
        copy.wait()
    for t in (2, 0, 1):
        wc(t, True).wait_recv()

    q_copy = remote(q.at[2], q.at[1], q_sem.at[0], q_sem.at[1], peers[2])
    tokens = gn[...].reshape(NZ * 32, gn.shape[2])

    @pl.loop(0, 2)
    def _(i):
        q[2 - 2 * i] = jnp.dot(tokens, w[1 - i, 2], preferred_element_type=F32).astype(BF16)

    q_copy.start()

    length = enc_len[0]

    def kv_copy(units, u):
        kv, ssem, rsem = ((kva, kva_send, kva_recv), (kvb, kvb_send, kvb_recv))[units]
        return remote(kv.at[2, u], kv.at[1, u], ssem.at[u], rsem.at[u], peers[2])

    def project(units, u, rows):
        kv = (kva, kvb)[units]
        for side in (2, 0):

            @pl.loop(0, 2)
            def _(which):
                kv[side, u, which] = jnp.dot(
                    rows, w[side // 2, which], preferred_element_type=F32
                ).astype(BF16)

            if side == 2:
                kv_copy(units, u).start()

    def attend(units, u, parts, last=False):
        kv = (kva, kvb)[units]
        n = 2 * kv.shape[3]
        kv_copy(units, u).wait_recv()
        keys = jnp.concatenate([kv[0, u, 0], kv[1, u, 0]], axis=0)
        values = jnp.concatenate([kv[0, u, 1], kv[1, u, 1]], axis=0)
        values_t = values.T
        index = []
        for row in (y, yn):
            for start, size in parts:
                index.append(lax.broadcasted_iota(jnp.int32, (size, 1), 0) + (row * NZ * 128 + start))
        valid = jnp.broadcast_to(jnp.concatenate(index, axis=0), (n, 512)) < length

        def head(h, v_h):
            s = jnp.dot(keys, qtm[h], preferred_element_type=F32)
            s = jnp.where(valid, s, NEG)
            old = mx[h]
            new = jnp.maximum(old, jnp.max(s, axis=0, keepdims=True))
            p = jnp.exp(s - new)
            scale = jnp.exp(old - new)
            total = scale * sm[h] + jnp.sum(p, axis=0, keepdims=True)
            summed = scale * acc[h] + jnp.dot(v_h, p.astype(BF16), preferred_element_type=F32)
            if last:
                return (summed * (1.0 / total)).astype(BF16)
            mx[h] = new
            sm[h] = total
            acc[h] = summed

        heads = [lambda h=h: head(h, values_t[64 * h : 64 * h + 64]) for h in range(4)]
        if last:
            return heads
        for run in heads:
            run()

    def pieces_of(units, u):
        if units:
            return [((z + 4) % NZ, u), ((z + 4) % NZ, u + 2)]
        late, near = u // 5, (u + 1) // 2
        block = (z + NZ + near - 2 * near * (u % 2)) % NZ
        sides = ((z + NZ - 3) % NZ, (z + 3) % NZ)
        return [
            ((1 - late) * block + late * sides[i // 2], (1 - late) * i + late * (2 * (u - 5) + i % 2))
            for i in range(4)
        ]

    def rows_of(units, u):
        parts = [
            gm[block, pl.ds(pl.multiple_of(32 * piece, 32), 32), :] for block, piece in pieces_of(units, u)
        ]
        return jnp.concatenate(parts, axis=0)

    def attend_unit(units, u, last=False):
        return attend(units, u, [(block * 128 + 32 * piece, 32) for block, piece in pieces_of(units, u)], last)

    before = {
        1: [(1, 7), (0, 8)],
        2: [(1, 8), (0, 9)],
        3: [(1, 9), (0, 10), (1, 10), (0, 11)],
        5: [(1, 11), (0, 12), (1, 12), (0, 13)],
        6: [(1, 13), (0, 14), (1, 14), (0, 15)],
    }

    @pl.loop(0, 7)
    def _(u):
        for at, todo in before.items():

            @pl.when(u == at)
            def _():
                for d, k in todo:
                    serve(d, k)

        @pl.when(u == 4)
        def _():
            got_xb(3)

        project(0, u, rows_of(0, u))

        @pl.when(u == 0)
        def _():
            q_copy.wait_recv()
            first = jnp.where(y == 0, q[0], q[1])
            second = jnp.where(y == 0, q[1], q[0])
            qt = jnp.concatenate([first.T, second.T], axis=1)
            column = lax.broadcasted_iota(jnp.int32, (256, 512), 0)
            for h in range(4):
                qtm[h] = jnp.where(column // HEAD_DIM == h, qt, jnp.zeros_like(qt))

        @pl.when(u > 0)
        def _():
            attend_unit(0, u - 1)

    serve(1, 15)
    serve(0, 16)
    project(1, 0, rows_of(1, 0))
    attend_unit(0, 6)
    serve(1, 16)
    serve(0, 17)
    serve(1, 17)
    project(1, 1, rows_of(1, 1))
    attend_unit(1, 0)

    heads = attend_unit(1, 1, True)

    def ctx_copy(pair):
        return remote(ctx.at[2, pair], ctx.at[1, pair], ctx_sem.at[0, pair], ctx_sem.at[1, pair], peers[2])

    for pair in (0, 1):
        full = jnp.concatenate([heads[2 * pair](), heads[2 * pair + 1]()], axis=0)
        low, high = full[:, :256].T, full[:, 256:].T
        ctx[2, pair] = jnp.where(y == 0, high, low)
        ctx_copy(pair).start()
        both_ctx[:, pl.ds(128 * pair, 128)] = jnp.where(y == 0, low, high)
    wc(3, True).wait_recv()
    for pair in (0, 1):
        ctx_copy(pair).wait_recv()
        both_ctx[:, pl.ds(256 + 128 * pair, 128)] = ctx[1, pair]

    orders = (
        [(0, 4), (1, 3), (0, 3), (1, 2), (0, 2), (1, 1), (0, 1)],
        [(1, 4), (0, 3), (1, 3), (0, 2), (1, 2), (0, 1), (1, 1)],
    )

    def rs_copy(d, i):
        return remote(rs_send.at[d, i], rs_recv.at[d, i], rss.at[d, i], rsr.at[d, i], peers[d])

    def term_of(owner, half):
        rows = both_ctx[pl.ds(pl.multiple_of(owner * 32, 32), 32), :]
        cols = pl.ds(half * 2048, 2048)
        return jnp.dot(rows[:, :256], wo[0, :, cols], preferred_element_type=F32) + jnp.dot(
            rows[:, 256:], wo[1, :, cols], preferred_element_type=F32
        )

    for i in range(7):
        for d in (0, 1):
            half, far = orders[d][i]
            term = term_of((z + (far if d == 0 else NZ - far)) % NZ, half)
            if i >= 2:
                rs_copy(d, i - 2).wait_recv()
                term = term + rs_recv[d, i - 2].astype(F32)
            rs_send[d, i] = term.astype(BF16)
            rs_copy(d, i).start()
    terms = [term_of(z, half) for half in (0, 1)]
    for d in (0, 1):
        for i in (5, 6):
            rs_copy(d, i).wait_recv()
    live = lax.broadcasted_iota(jnp.int32, (32, 2048), 0) + (y * NZ + z) * 32 < dec_len[0]
    for half in (0, 1):
        total = terms[half] + rs_recv[0, 6 - half].astype(F32) + rs_recv[1, 5 + half].astype(F32)
        out_ref[:, pl.ds(half * 2048, 2048)] = jnp.where(live, total, 0.0).astype(BF16)

    for d in (0, 1):
        for i in range(len((R_ITEMS, L_ITEMS)[d])):
            z_copy(d, i, False).wait_send()
        for i in range(7):
            rs_copy(d, i).wait_send()
    for t in range(4):
        wy(t).wait_send()
        wxa(t).wait_send()
        wxb(t, 0).wait_send()
        wxb(t, 1).wait_send()
        wc(t).wait_send()
    q_copy.wait_send()
    for pair in (0, 1):
        ctx_copy(pair).wait_send()
    for u in range(7):
        kv_copy(0, u).wait_send()
    for u in range(2):
        kv_copy(1, u).wait_send()


def shards(enc_hidden, enc_gain, dec_hidden, dec_gain, w_query, w_key, w_value, w_out, enc_length, dec_length):
    width = w_query.shape[0]
    rows = dec_hidden.shape[0]
    anywhere = pl.BlockSpec(memory_space=pl.ANY)
    dma = pltpu.SemaphoreType.DMA
    return pl.pallas_call(
        kernel,
        out_shape=(
            pltpu.VMEM(enc_hidden.shape, BF16),
            pltpu.VMEM((rows, width), BF16),
        ),
        in_specs=[anywhere] * 10,
        out_specs=(pl.BlockSpec(memory_space=pltpu.VMEM), pl.BlockSpec(memory_space=pltpu.VMEM)),
        scratch_shapes=[
            pltpu.SMEM((1,), jnp.int32),
            pltpu.SMEM((1,), jnp.int32),
            pltpu.VMEM((160, width), BF16),
            pltpu.VMEM((2, 1, width), F32),
            pltpu.VMEM((NZ, 32, width), BF16),
            pltpu.VMEM((NZ, 128, width), BF16),
            pltpu.VMEM((2, 3, width, 256), BF16),
            pltpu.VMEM((2, 256, width), BF16),
            pltpu.VMEM((3, 7, 2, 128, 256), BF16),
            pltpu.VMEM((3, 2, 2, 64, 256), BF16),
            pltpu.VMEM((3, 256, 256), BF16),
            pltpu.VMEM((4, 256, 512), BF16),
            pltpu.VMEM((4, 64, 512), F32),
            pltpu.VMEM((4, 1, 512), F32),
            pltpu.VMEM((4, 1, 512), F32),
            pltpu.VMEM((3, 2, 256, 128), BF16),
            pltpu.VMEM((256, 512), BF16),
            pltpu.VMEM((2, 7, 32, width // 2), BF16),
            pltpu.VMEM((2, 7, 32, width // 2), BF16),
            dma((11,)),
            dma((2, 18)),
            dma((2, 18)),
            dma((4,)),
            dma((4,)),
            dma((4,)),
            dma((4,)),
            dma((4, 2)),
            dma((4, 2)),
            dma((4,)),
            dma((4,)),
            dma((2,)),
            dma((2, 2)),
            dma((7,)),
            dma((7,)),
            dma((2,)),
            dma((2,)),
            dma((2, 7)),
            dma((2, 7)),
        ],
        compiler_params=pltpu.CompilerParams(
            collective_id=0, has_side_effects=True, vmem_limit_bytes=60 * 1024 * 1024
        ),
        name="cross_attention",
    )(
        enc_length,
        dec_length,
        enc_hidden,
        enc_gain.reshape(1, width),
        dec_hidden,
        dec_gain.reshape(1, width),
        w_query,
        w_key,
        w_value,
        w_out,
    )


def solution(mesh):
    torus = Mesh(mesh.devices.reshape(4, 2, 2, 2, NZ), ROWS)
    tensor = ("yl", "z")
    dp = ("x", "yh", "c")
    in_specs = (
        P(ROWS, None),
        P(),
        P(ROWS, None),
        P(),
        P(None, tensor),
        P(None, tensor),
        P(None, tensor),
        P(tensor, None),
        P(dp),
        P(dp),
    )
    out_specs = (P(ROWS, None), P(ROWS, None))
    return jax.shard_map(shards, mesh=torus, in_specs=in_specs, out_specs=out_specs, check_vma=False)
```

time: 159 us -> 147 us (0.925)
  Pallas kernels: 150 us -> 143 us
  other arithmetic: 6.86 us -> 0 us
  local copies, waits for them, and re-layouts: 0.01 us -> 1.67 us
    pallas_call x1, Pallas kernels: 150 us -> 143 us  [shards(): pl.pallas_call(kernel, out_shape=(pltpu.VMEM(enc_hidden.shape, BF16), plt...]
    convert_element_type x2 -> x0, other arithmetic: 3.36 us -> none  [rms_norm(): return (wide * lax.rsqrt(mean_sq + 1e-06) * gain).astype(BF16)]
    select_n x1 -> x0, other arithmetic: 1.74 us -> none  [shards(): jnp.where((row_ids < dec_length[0])[:, None], summed, jnp.zeros_like(summ...]
    reduce_sum x2 -> x0, other arithmetic: 1.73 us -> none  [rms_norm(): mean_sq = jnp.mean(wide * wide, axis=-1, keepdims=True)]
    unnamed x4 -> x2, local copies, waits for them, and re-layouts: 0.01 us -> 1.67 us
where the time goes in v2:
time: 147 us; the launch traced here: 146 us
  Pallas kernels  143 us (97%)
  between operations  1.93 us (1%)
  local copies, waits for them, and re-layouts  1.67 us (1%)
    pallas_call x1, Pallas kernels, shards(): pl.pallas_call(kernel, out_shape=(pltpu.VMEM(enc_hidden.shape, BF16), plt...  143 us

profile of v2, /device:TPU:8, one launch (start us, length us, event | category | flops | bytes accessed | tf_op | source)
XLA Modules:
  0.0 146.2 jit_solution(4220705835232827659)
XLA Ops:
  1.9 142.6 %cross_attention.1 = (bf16[128,4096]{1,0:T(8,128)(2,1)S(1)}, bf16[32,4096]{1,0:T(8,128)(2,1)S(1)}) custom-call(s32[1]{0:T(128)S(6)} %copy.16.enc_len_hbm, s32[1]{0:T(128)S(6)} %copy.17.dec_len_hbm, bf16[128,4096]{1,0:T(8,128)(2,1)} %enc_hbm.1, f32[1,4096]{1,0:T(1,128)} %bitcast.2, bf16[32,4096]{1,0:T(8,128)(2,1)} %dec_hbm.1, f32[1,4096]{1,0:T(1,128)} %bitcast.3, ...), custom_call_target="tpu_custom_call" | custom-call | tf_op jit(solution)/shard_map/cross_attention/pallas_call | solution.py:405
  144.5 1.0 copy.14
  145.5 0.7 copy.15

commit v3 on v2

v3 whole, which is shorter than its diff:
```python
import functools

import jax
import jax.numpy as jnp
from jax import lax
from jax.experimental import pallas as pl
from jax.experimental.pallas import tpu as pltpu
from jax.sharding import Mesh
from jax.sharding import PartitionSpec as P

HEAD_DIM = 64
MESH = pl.DeviceIdType.MESH
NZ = 8
NEG = -1e30
ROWS = ("x", "yh", "c", "yl", "z")
BF16, F32 = jnp.bfloat16, jnp.float32

OUTER = (
    [("n", 0, 0), ("m", 0, 0), ("n", 1, 0), ("m", 0, 1), ("n", 2, 0), ("m", 0, 2), ("n", 3, 4), ("m", 0, 3)]
    + [("m", 1, p) for p in range(4)]
    + [("m", 2, p) for p in range(4)]
)
INNER = (
    [("n", 0, 0), ("w", 0, 0), ("n", 1, 0), ("w", 0, 1), ("n", 2, 0), ("m", 0, 0), ("n", 3, 5)]
    + [("m", 0, p) for p in (1, 2, 3)]
    + [("m", 1, p) for p in range(4)]
)
ITEMS = (OUTER, INNER)


def schedule(d):
    after, last = {}, -1
    for i, (kind, hop, piece) in enumerate(ITEMS[d]):
        if hop:
            last = max(last, ITEMS[1 - d].index((kind, hop - 1, piece % 4 if kind == "m" else 0)))
        after.setdefault(last, []).append(i)
    return after


def rms_norm(values, gain):
    wide = values.astype(F32)
    mean_sq = jnp.mean(wide * wide, axis=-1, keepdims=True)
    return (wide * lax.rsqrt(mean_sq + 1e-06) * gain).astype(BF16)


def kernel(
    enc_len_hbm, dec_len_hbm, enc_hbm, encg_hbm, dec_hbm, decg_hbm, wq_hbm, wk_hbm, wv_hbm, wo_hbm, mem_out, out_ref,
    enc_len, dec_len, raw, gain, gn, gm, w, w2, wo, kva, kvb, kvc, q, qtm, acc, mx, sm, ctx, both_ctx, rs_send, rs_recv,
    ready, loc, z_send, z_recv, wy_send, wy_recv, xa_send, xa_recv, xb_send, xb_recv, c_send, c_recv,
    q_sem, ctx_sem, kva_send, kva_recv, kvb_send, kvb_recv, kvc_send, kvc_recv, as_send, as_recv, rss, rsr,
):
    x, c = lax.axis_index("x"), lax.axis_index("c")
    y, z = lax.axis_index("yl"), lax.axis_index("z")
    yh = lax.axis_index("yh")
    yn, cn = 1 - y, 1 - c
    xa, xb = x + 1 - 2 * (x % 2), 3 - x
    right, left = (z + 1) % NZ, (z + NZ - 1) % NZ
    sign = 1 - 2 * (z % 2)
    inner, outer = z + sign, (z + NZ - sign) % NZ
    ring = ({"z": right}, {"z": left})
    peers = ({"z": outer}, {"z": inner}, {"yl": yn}, {"x": xa}, {"x": xb}, {"c": cn}, {"yl": yn, "z": inner})
    peers += ({"yl": yn, "yh": 1 - yh},)

    barrier = pltpu.get_barrier_semaphore()

    def greet(*to):
        for peer in to:
            pl.semaphore_signal(barrier, inc=1, device_id=peer, device_id_type=MESH)

    def answer(which, peer):
        pl.semaphore_signal(ready.at[which], inc=1, device_id=peer, device_id_type=MESH)

    greet(*peers[:3], *peers[6:])
    pl.when(c == 0)(lambda: greet(peers[5]))
    pl.when(x == 0)(lambda: greet(peers[3], peers[4]))
    pl.when(x == 1)(lambda: greet(peers[4]))
    pl.when(x == 3)(lambda: greet(peers[3]))

    enters = [
        pltpu.make_async_copy(dec_hbm, raw.at[pl.ds(0, 32), :], loc.at[0]),
        pltpu.make_async_copy(decg_hbm, gain.at[0], loc.at[1]),
        pltpu.make_async_copy(enc_hbm, raw.at[pl.ds(32, 128), :], loc.at[2]),
        pltpu.make_async_copy(encg_hbm, gain.at[1], loc.at[3]),
    ]
    local = [
        pltpu.make_async_copy(wk_hbm, w.at[0, 0], loc.at[4]),
        pltpu.make_async_copy(wv_hbm, w.at[0, 1], loc.at[5]),
        pltpu.make_async_copy(wq_hbm, w.at[0, 2], loc.at[6]),
        pltpu.make_async_copy(wo_hbm, wo.at[0], loc.at[7]),
        pltpu.make_async_copy(enc_len_hbm, enc_len, loc.at[9]),
        pltpu.make_async_copy(dec_len_hbm, dec_len, loc.at[10]),
    ]
    for copy in enters + local:
        copy.start()
    enters[0].wait()
    enters[1].wait()
    gn[z] = rms_norm(raw[pl.ds(0, 32), :], gain[0])
    enters[2].wait()
    enters[3].wait()

    def norm_piece(p):
        gm[z, pl.ds(32 * p, 32), :] = rms_norm(raw[pl.ds(32 + 32 * p, 32), :], gain[1])

    norm_piece(0)
    pl.semaphore_wait(barrier, 5 + c + x - 2 * (x // 3))

    def remote(src, dst, ssem, rsem, peer):
        return pltpu.make_async_remote_copy(
            src_ref=src, dst_ref=dst, send_sem=ssem, recv_sem=rsem, device_id=peer, device_id_type=MESH
        )

    hbm = (wk_hbm, wv_hbm, wq_hbm, wo_hbm)

    def partner_of(t, at):
        return at + 1 - 2 * (at % 2) if t in (1, 3, 4, 6) else 3 - at

    def held(t, at, other=False):
        flip = 1 - yh if other else yh
        return c * 4 + at + flip * (partner_of(t, at) - at)


    def part(t, e, n=1):
        if t == 3:
            return wo.at[1, pl.ds(e * 32, n * 32), :]
        rows = pl.ds(e * 512, n * 512)
        return w.at[1, t, rows, :] if t < 3 else w2.at[t // 2 - 2, t % 2, rows, :]

    def z_ref(kind, owner, piece):
        if kind == "n":
            return gn.at[owner] if piece == 0 else gn.at[owner, pl.ds(16 * (piece - 4), 16), :]
        return gm.at[owner, pl.ds(32 * piece, 32), :]

    def z_copy(d, i, receive):
        kind, hop, piece = ITEMS[d][i]
        if kind == "w":
            e = held(4 + piece, x)
            src, dst = hbm[piece].at[pl.ds(e * 512, 512), :], part(4 + piece, e)
        else:
            away = sign if d == (1 if receive else 0) else -sign
            src = dst = z_ref(kind, (z + NZ + away * (hop + (1 if receive else 0))) % NZ, piece)
        return remote(src, dst, z_send.at[d, i], z_recv.at[d, i], peers[d])

    plan = (schedule(0), schedule(1))

    def z_issue(d, k):
        for i in plan[d].get(k, ()):
            z_copy(d, i, False).start()

    def serve(d, k):
        z_copy(d, k, True).wait_recv()
        z_issue(1 - d, k)

    def wy(t, far, receive=False):
        e = held(t, x, receive and far == 1)
        size = 32 if t == 3 else 512
        src = hbm[t].at[pl.ds(e * size, size), :] if t < 4 else part(t - 2, e)
        return remote(src, part(t, e), wy_send.at[t, far], wy_recv.at[t, far], peers[7 if far else 2])

    def wx(t, k, receive=False):
        if t in (4, 5):
            near, at, peer = ((xa, xb, 4), (xb, xa, 3))[t - 4]
            e = held(t, (3 - xa if k else at) if receive else (near if k else x))
        else:
            at, peer = (xb, 4) if t in (1, 3, 6) else (xa, 3)
            e = held(t, at if receive else x, k == 1)
        return remote(part(t, e), part(t, e), xb_send.at[t, k], xb_recv.at[t, k], peers[peer])

    def wnear(t, receive=False):
        at, peer = ((xa, 3), (xb, 4))[t - 4]
        r = part(t, held(t, at if receive else x))
        return remote(r, r, xa_send.at[t], xa_recv.at[t], peers[peer])

    def wc(t, receive=False):
        r = part(t, 4 * (cn if receive else c), 4)
        return remote(r, r, c_send.at[t], c_recv.at[t], peers[5])

    def send_y(t):
        wy(t, 0).start()
        wy(t, 1).start()

    def got_y(t):
        for k in (0, 1):
            wy(t, k, True).wait_recv()
        for k in (0, 1):
            wx(t, k).start()

    def got_z(t):
        send_y(t + 2)
        wx(t, 0).start()
        wnear(t).start()

    def got_near(t):
        wnear(t, True).wait_recv()
        wx(t, 1).start()

    def got_x(t):
        for k in (0, 1):
            wx(t, k, True).wait_recv()
        wc(t).start()

    for d in (0, 1):
        z_issue(d, -1)
    for t in range(3):
        send_y(t)
    pl.when(c == 1)(lambda: answer(0, peers[5]))
    pl.when(x == 1)(lambda: answer(1, peers[3]))
    pl.when(x == 3)(lambda: answer(2, peers[4]))

    @pl.when(x == 2)
    def _():
        answer(1, peers[3])
        answer(2, peers[4])
    @pl.loop(1, 4)
    def _(p):
        norm_piece(p)

    mem_out[...] = gm[z]
    mx[...] = jnp.full_like(mx, NEG)
    sm[...] = jnp.zeros_like(sm)
    acc[...] = jnp.zeros_like(acc)

    def both(k):
        serve(0, k)
        serve(1, k)

    both(0)

    @pl.when(x // 2 == 0)
    def _():
        pl.semaphore_wait(ready.at[2], 1)

    pl.when(x % 3 == 0)(lambda: pl.semaphore_wait(ready.at[1], 1))
    got_y(0)
    got_y(1)
    both(1)
    got_z(4)
    got_y(2)
    both(2)
    both(3)
    got_z(5)
    send_y(3)
    got_y(6)
    pl.when(c == 0)(lambda: pl.semaphore_wait(ready.at[0], 1))
    got_x(0)
    got_near(4)
    both(4)
    got_x(1)
    got_y(7)
    both(5)
    got_x(2)
    both(6)
    serve(0, 7)
    for copy in local:
        copy.wait()
    for t in (2, 0, 1):
        wc(t, True).wait_recv()

    q_copy = remote(q.at[2], q.at[1], q_sem.at[0], q_sem.at[1], peers[2])
    tokens = gn[...].reshape(NZ * 32, gn.shape[2])

    @pl.loop(0, 2)
    def _(i):
        q[2 - 2 * i] = jnp.dot(tokens, w[1 - i, 2], preferred_element_type=F32).astype(BF16)

    q_copy.start()

    length = enc_len[0]

    kvs, seen = (kva, kvb, kvc), (5, 1, 1)
    kv_sems = ((kva_send, kva_recv), (kvb_send, kvb_recv), (kvc_send, kvc_recv))

    def kv_copy(units, u):
        kv, (ssem, rsem) = kvs[units], kv_sems[units]
        return remote(kv.at[2, u], kv.at[1, u], ssem.at[u], rsem.at[u], peers[2])

    def help_copy(units, side):
        kv, there = kvs[units], seen[units]
        return remote(
            kv.at[side, there + 1],
            kv.at[side, there],
            as_send.at[units, side],
            as_recv.at[units, side],
            peers[6 if side else 1],
        )

    def project(units, u, rows, sides=(2, 0)):
        kv = kvs[units]
        for side in sides:

            @pl.loop(0, 2)
            def _(which):
                kv[side, u, which] = jnp.dot(
                    rows, w[side // 2, which], preferred_element_type=F32
                ).astype(BF16)

            if side == 2:
                kv_copy(units, u).start()

    def assist(units, rows):
        kv, here = kvs[units], seen[units] + 1
        for side in (1, 0):

            @pl.loop(0, 2)
            def _(which):
                kv[side, here, which] = jnp.dot(rows, w2[side, which], preferred_element_type=F32).astype(BF16)

            help_copy(units, side).start()

    def attend(slots, last=False):
        keys, values, index = [], [], []
        for units, u, block, start in slots:
            kv = kvs[units]
            if not isinstance(u, int) or u < seen[units]:
                kv_copy(units, u).wait_recv()
            else:
                help_copy(units, 0).wait_recv()
                help_copy(units, 1).wait_recv()
            for side, row in ((0, y), (1, yn)):
                size = kv.shape[3]
                keys.append(kv[side, u, 0])
                values.append(kv[side, u, 1])
                base = (row * NZ + block) * 128 + start
                index.append(lax.broadcasted_iota(jnp.int32, (size, 1), 0) + base)
        keys = jnp.concatenate(keys, axis=0)
        values_t = jnp.concatenate(values, axis=0).T
        valid = jnp.broadcast_to(jnp.concatenate(index, axis=0), (keys.shape[0], 512)) < length

        def head(h, v_h):
            s = jnp.dot(keys, qtm[h], preferred_element_type=F32)
            s = jnp.where(valid, s, NEG)
            old = mx[h]
            new = jnp.maximum(old, jnp.max(s, axis=0, keepdims=True))
            p = jnp.exp(s - new)
            scale = jnp.exp(old - new)
            total = scale * sm[h] + jnp.sum(p, axis=0, keepdims=True)
            summed = scale * acc[h] + jnp.dot(v_h, p.astype(BF16), preferred_element_type=F32)
            if last:
                return (summed * (1.0 / total)).astype(BF16)
            mx[h] = new
            sm[h] = total
            acc[h] = summed

        heads = [lambda h=h: head(h, values_t[64 * h : 64 * h + 64]) for h in range(4)]
        if last:
            return heads
        for run in heads:
            run()

    def block_of(u):
        return (z + NZ + sign * ((u + 1) // 2) * (1 - 2 * (u % 2))) % NZ

    ends = {1: (0, 96), 2: (96, 32)}

    def end_rows(units):
        return gm[(z + NZ - 3 * sign) % NZ, pl.ds(*ends[units]), :]

    def end_slots(units):
        start = ends[units][0]
        return [(units, 0, (z + NZ - 3 * sign) % NZ, start), (units, 1, (z + 4) % NZ, start)]

    before = {
        1: lambda: (serve(1, 7), got_near(5), got_y(3)),
        2: lambda: (serve(1, 8), serve(0, 8), got_x(6), got_x(4), serve(1, 9), serve(0, 9)),
        3: lambda: (serve(0, 10), serve(1, 10), got_x(7), got_x(5), serve(0, 11), serve(1, 11)),
    }

    @pl.loop(0, 4)
    def _(u):
        for at, take in before.items():

            @pl.when(u == at)
            def _():
                take()

        project(0, u, gm[block_of(u)])

        @pl.when(u == 0)
        def _():
            q_copy.wait_recv()
            first = jnp.where(y == 0, q[0], q[1])
            second = jnp.where(y == 0, q[1], q[0])
            qt = jnp.concatenate([first.T, second.T], axis=1)
            column = lax.broadcasted_iota(jnp.int32, (256, 512), 0)
            for h in range(4):
                qtm[h] = jnp.where(column // HEAD_DIM == h, qt, jnp.zeros_like(qt))

        attend([(0, u, block_of(u), 0)])

    serve(1, 12)
    serve(0, 12)
    for t in (4, 5, 6, 7):
        wc(t, True).wait_recv()
    assist(0, gm[block_of(3)])
    serve(1, 13)
    serve(0, 13)
    got_x(3)
    project(0, 4, gm[block_of(4)])
    attend([(0, 5, (z + NZ + 3 * sign) % NZ, 0)])
    attend([(0, 4, block_of(4), 0)])
    serve(0, 14)
    rows = end_rows(1)
    assist(1, rows)
    project(1, 0, rows)
    serve(0, 15)
    rows = end_rows(2)
    assist(2, rows)
    project(2, 0, rows, (2,))
    attend(end_slots(1))
    project(2, 0, rows, (0,))

    heads = attend(end_slots(2), True)

    def ctx_copy(pair):
        return remote(ctx.at[2, pair], ctx.at[1, pair], ctx_sem.at[0, pair], ctx_sem.at[1, pair], peers[2])

    for pair in (0, 1):
        full = jnp.concatenate([heads[2 * pair](), heads[2 * pair + 1]()], axis=0)
        low, high = full[:, :256].T, full[:, 256:].T
        ctx[2, pair] = jnp.where(y == 0, high, low)
        ctx_copy(pair).start()
        both_ctx[:, pl.ds(128 * pair, 128)] = jnp.where(y == 0, low, high)
    wc(3, True).wait_recv()
    for pair in (0, 1):
        ctx_copy(pair).wait_recv()
        both_ctx[:, pl.ds(256 + 128 * pair, 128)] = ctx[1, pair]

    orders = []
    for long in ((0, 1), (2, 3)):
        short = (2, 3) if long[0] == 0 else (0, 1)
        order = [(quarter, 4) for quarter in long]
        for far in (3, 2, 1):
            order += [(quarter, far) for quarter in short + long]
        orders.append(order)
    n_rs = len(orders[0])

    def rs_copy(d, i):
        return remote(rs_send.at[d, i], rs_recv.at[d, i], rss.at[d, i], rsr.at[d, i], ring[d])

    def term_of(owner, quarter):
        rows = both_ctx[pl.ds(pl.multiple_of(owner * 32, 32), 32), :]
        cols = pl.ds(quarter * 1024, 1024)
        return jnp.dot(rows[:, :256], wo[0, :, cols], preferred_element_type=F32) + jnp.dot(
            rows[:, 256:], wo[1, :, cols], preferred_element_type=F32
        )

    for i in range(n_rs):
        for d in (0, 1):
            quarter, far = orders[d][i]
            term = term_of((z + (far if d == 0 else NZ - far)) % NZ, quarter)
            if (quarter, far + 1) in orders[d]:
                k = orders[d].index((quarter, far + 1))
                rs_copy(d, k).wait_recv()
                term = term + rs_recv[d, k].astype(F32)
            rs_send[d, i] = term.astype(BF16)
            rs_copy(d, i).start()
    terms = [term_of(z, quarter) for quarter in range(4)]
    live = lax.broadcasted_iota(jnp.int32, (32, 1024), 0) + (y * NZ + z) * 32 < dec_len[0]
    for i in range(n_rs - 4, n_rs):
        for d in (0, 1):
            rs_copy(d, i).wait_recv()
            quarter = orders[d][i][0]
            terms[quarter] = terms[quarter] + rs_recv[d, i].astype(F32)
    for quarter in range(4):
        out_ref[:, pl.ds(quarter * 1024, 1024)] = jnp.where(live, terms[quarter], 0.0).astype(BF16)

    for d in (0, 1):
        for i in range(len(ITEMS[d])):
            z_copy(d, i, False).wait_send()
        for i in range(n_rs):
            rs_copy(d, i).wait_send()
    for t in range(8):
        for k in (0, 1):
            if t not in (4, 5):
                wy(t, k).wait_send()
            wx(t, k).wait_send()
        if t in (4, 5):
            wnear(t).wait_send()
        wc(t).wait_send()
    q_copy.wait_send()
    for pair in (0, 1):
        ctx_copy(pair).wait_send()
    for u in range(5):
        kv_copy(0, u).wait_send()
    for units in (1, 2):
        kv_copy(units, 0).wait_send()
    for units in range(3):
        for side in (0, 1):
            help_copy(units, side).wait_send()


def shards(enc_hidden, enc_gain, dec_hidden, dec_gain, w_query, w_key, w_value, w_out, enc_length, dec_length):
    width = w_query.shape[0]
    rows = dec_hidden.shape[0]
    anywhere = pl.BlockSpec(memory_space=pl.ANY)
    dma = pltpu.SemaphoreType.DMA
    return pl.pallas_call(
        kernel,
        out_shape=(
            pltpu.VMEM(enc_hidden.shape, BF16),
            pltpu.VMEM((rows, width), BF16),
        ),
        in_specs=[anywhere] * 10,
        out_specs=(pl.BlockSpec(memory_space=pltpu.VMEM), pl.BlockSpec(memory_space=pltpu.VMEM)),
        scratch_shapes=[
            pltpu.SMEM((1,), jnp.int32),
            pltpu.SMEM((1,), jnp.int32),
            pltpu.VMEM((160, width), BF16),
            pltpu.VMEM((2, 1, width), F32),
            pltpu.VMEM((NZ, 32, width), BF16),
            pltpu.VMEM((NZ, 128, width), BF16),
            pltpu.VMEM((2, 3, width, 256), BF16),
            pltpu.VMEM((2, 2, width, 256), BF16),
            pltpu.VMEM((2, 256, width), BF16),
            pltpu.VMEM((3, 7, 2, 128, 256), BF16),
            pltpu.VMEM((3, 3, 2, 96, 256), BF16),
            pltpu.VMEM((3, 3, 2, 32, 256), BF16),
            pltpu.VMEM((3, 256, 256), BF16),
            pltpu.VMEM((4, 256, 512), BF16),
            pltpu.VMEM((4, 64, 512), F32),
            pltpu.VMEM((4, 1, 512), F32),
            pltpu.VMEM((4, 1, 512), F32),
            pltpu.VMEM((3, 2, 256, 128), BF16),
            pltpu.VMEM((256, 512), BF16),
            pltpu.VMEM((2, 14, 32, width // 4), BF16),
            pltpu.VMEM((2, 14, 32, width // 4), BF16),
            pltpu.SemaphoreType.REGULAR((3,)),
            dma((11,)),
            dma((2, 16)),
            dma((2, 16)),
            dma((8, 2)),
            dma((8, 2)),
            dma((8,)),
            dma((8,)),
            dma((8, 2)),
            dma((8, 2)),
            dma((8,)),
            dma((8,)),
            dma((2,)),
            dma((2, 2)),
            dma((5,)),
            dma((5,)),
            dma((1,)),
            dma((1,)),
            dma((1,)),
            dma((1,)),
            dma((3, 2)),
            dma((3, 2)),
            dma((2, 14)),
            dma((2, 14)),
        ],
        compiler_params=pltpu.CompilerParams(
            collective_id=0, has_side_effects=True, vmem_limit_bytes=60 * 1024 * 1024
        ),
        name="cross_attention",
    )(
        enc_length,
        dec_length,
        enc_hidden,
        enc_gain.reshape(1, width),
        dec_hidden,
        dec_gain.reshape(1, width),
        w_query,
        w_key,
        w_value,
        w_out,
    )


def solution(mesh):
    torus = Mesh(mesh.devices.reshape(4, 2, 2, 2, NZ), ROWS)
    tensor = ("yl", "z")
    dp = ("x", "yh", "c")
    in_specs = (
        P(ROWS, None),
        P(),
        P(ROWS, None),
        P(),
        P(None, tensor),
        P(None, tensor),
        P(None, tensor),
        P(tensor, None),
        P(dp),
        P(dp),
    )
    out_specs = (P(ROWS, None), P(ROWS, None))
    return jax.shard_map(shards, mesh=torus, in_specs=in_specs, out_specs=out_specs, check_vma=False)
```

time: 147 us -> 140 us (0.952)
  Pallas kernels: 143 us -> 135 us
    pallas_call x1, Pallas kernels: 143 us -> 135 us  [shards(): pl.pallas_call(kernel, out_shape=(pltpu.VMEM(enc_hidden.shape, BF16), plt...]
where the time goes in v3:
time: 140 us; the launch traced here: 138 us
  Pallas kernels  135 us (96%)
  between operations  1.93 us (1%)
  local copies, waits for them, and re-layouts  1.67 us (1%)
    pallas_call x1, Pallas kernels, shards(): pl.pallas_call(kernel, out_shape=(pltpu.VMEM(enc_hidden.shape, BF16), plt...  135 us

profile of v3, /device:TPU:8, one launch (start us, length us, event | category | flops | bytes accessed | tf_op | source)
XLA Modules:
  0.0 138.5 jit_solution(3457979328632073019)
XLA Ops:
  1.9 134.8 %cross_attention.1 = (bf16[128,4096]{1,0:T(8,128)(2,1)S(1)}, bf16[32,4096]{1,0:T(8,128)(2,1)S(1)}) custom-call(s32[1]{0:T(128)S(6)} %copy.16.enc_len_hbm, s32[1]{0:T(128)S(6)} %copy.17.dec_len_hbm, bf16[128,4096]{1,0:T(8,128)(2,1)} %enc_hbm.1, f32[1,4096]{1,0:T(1,128)} %bitcast.2, bf16[32,4096]{1,0:T(8,128)(2,1)} %dec_hbm.1, f32[1,4096]{1,0:T(1,128)} %bitcast.3, ...), custom_call_target="tpu_custom_call" | custom-call | tf_op jit(solution)/shard_map/cross_attention/pallas_call | solution.py:496
  136.8 1.0 copy.14
  137.8 0.7 copy.15

commit v4 on v3

--- a/solution.py
+++ b/solution.py
@@ -249,6 +249,7 @@
     both(5)
     got_x(2)
     both(6)
+    got_near(5)
     serve(0, 7)
     for copy in local:
         copy.wait()
@@ -359,9 +360,9 @@
         return [(units, 0, (z + NZ - 3 * sign) % NZ, start), (units, 1, (z + 4) % NZ, start)]
 
     before = {
-        1: lambda: (serve(1, 7), got_near(5), got_y(3)),
-        2: lambda: (serve(1, 8), serve(0, 8), got_x(6), got_x(4), serve(1, 9), serve(0, 9)),
-        3: lambda: (serve(0, 10), serve(1, 10), got_x(7), got_x(5), serve(0, 11), serve(1, 11)),
+        1: lambda: (serve(1, 7), got_y(3), got_x(6)),
+        2: lambda: (serve(1, 8), serve(0, 8), got_x(4), serve(1, 9), serve(0, 9), got_x(7)),
+        3: lambda: (got_x(5), serve(0, 10), serve(1, 10), serve(0, 11), serve(1, 11)),
     }
 
     @pl.loop(0, 4)
@@ -384,13 +385,16 @@
             for h in range(4):
                 qtm[h] = jnp.where(column // HEAD_DIM == h, qt, jnp.zeros_like(qt))
 
-        attend([(0, u, block_of(u), 0)])
+        @pl.when(u > 0)
+        def _():
+            attend([(0, u - 1, block_of(u - 1), 0)])
 
     serve(1, 12)
     serve(0, 12)
     for t in (4, 5, 6, 7):
         wc(t, True).wait_recv()
     assist(0, gm[block_of(3)])
+    attend([(0, 3, block_of(3), 0)])
     serve(1, 13)
     serve(0, 13)
     got_x(3)

time: 140 us -> 136 us (0.971)
  Pallas kernels: 135 us -> 132 us
    pallas_call x1, Pallas kernels: 135 us -> 132 us  [shards(): pl.pallas_call(kernel, out_shape=(pltpu.VMEM(enc_hidden.shape, BF16), plt...]
where the time goes in v4:
time: 136 us
  Pallas kernels  132 us (97%)
  between operations  1.93 us (1%)
  local copies, waits for them, and re-layouts  1.67 us (1%)
    pallas_call x1, Pallas kernels, shards(): pl.pallas_call(kernel, out_shape=(pltpu.VMEM(enc_hidden.shape, BF16), plt...  132 us

profile of v4, /device:TPU:8, one launch (start us, length us, event | category | flops | bytes accessed | tf_op | source)
XLA Modules:
  0.0 135.7 jit_solution(7631182055725610679)
XLA Ops:
  1.9 132.0 %cross_attention.1 = (bf16[128,4096]{1,0:T(8,128)(2,1)S(1)}, bf16[32,4096]{1,0:T(8,128)(2,1)S(1)}) custom-call(s32[1]{0:T(128)S(6)} %copy.16.enc_len_hbm, s32[1]{0:T(128)S(6)} %copy.17.dec_len_hbm, bf16[128,4096]{1,0:T(8,128)(2,1)} %enc_hbm.1, f32[1,4096]{1,0:T(1,128)} %bitcast.2, bf16[32,4096]{1,0:T(8,128)(2,1)} %dec_hbm.1, f32[1,4096]{1,0:T(1,128)} %bitcast.3, ...), custom_call_target="tpu_custom_call" | custom-call | tf_op jit(solution)/shard_map/cross_attention/pallas_call | solution.py:500
  134.0 1.0 copy.14
  134.9 0.7 copy.15

commit v5 on v4

--- a/solution.py
+++ b/solution.py
@@ -79,8 +79,9 @@
     enters = [
         pltpu.make_async_copy(dec_hbm, raw.at[pl.ds(0, 32), :], loc.at[0]),
         pltpu.make_async_copy(decg_hbm, gain.at[0], loc.at[1]),
-        pltpu.make_async_copy(enc_hbm, raw.at[pl.ds(32, 128), :], loc.at[2]),
+        pltpu.make_async_copy(enc_hbm.at[pl.ds(0, 32), :], raw.at[pl.ds(32, 32), :], loc.at[2]),
         pltpu.make_async_copy(encg_hbm, gain.at[1], loc.at[3]),
+        pltpu.make_async_copy(enc_hbm.at[pl.ds(32, 96), :], raw.at[pl.ds(64, 96), :], loc.at[8]),
     ]
     local = [
         pltpu.make_async_copy(wk_hbm, w.at[0, 0], loc.at[4]),
@@ -90,7 +91,7 @@
         pltpu.make_async_copy(enc_len_hbm, enc_len, loc.at[9]),
         pltpu.make_async_copy(dec_len_hbm, dec_len, loc.at[10]),
     ]
-    for copy in enters + local:
+    for copy in enters:
         copy.start()
     enters[0].wait()
     enters[1].wait()
@@ -210,6 +211,10 @@
     def _():
         answer(1, peers[3])
         answer(2, peers[4])
+    for copy in local:
+        copy.start()
+    enters[4].wait()
+
     @pl.loop(1, 4)
     def _(p):
         norm_piece(p)

time: 136 us -> 136 us (level)
  no operation moved by 1% of the time
where the time goes in v5:
time: 136 us
  Pallas kernels  132 us (97%)
  between operations  1.93 us (1%)
  local copies, waits for them, and re-layouts  1.67 us (1%)
    pallas_call x1, Pallas kernels, shards(): pl.pallas_call(kernel, out_shape=(pltpu.VMEM(enc_hidden.shape, BF16), plt...  132 us

profile of v5, /device:TPU:8, one launch (start us, length us, event | category | flops | bytes accessed | tf_op | source)
XLA Modules:
  0.0 135.9 jit_solution(16910473075004926352)
XLA Ops:
  1.9 132.2 %cross_attention.1 = (bf16[128,4096]{1,0:T(8,128)(2,1)S(1)}, bf16[32,4096]{1,0:T(8,128)(2,1)S(1)}) custom-call(s32[1]{0:T(128)S(6)} %copy.16.enc_len_hbm, s32[1]{0:T(128)S(6)} %copy.17.dec_len_hbm, bf16[128,4096]{1,0:T(8,128)(2,1)} %enc_hbm.1, f32[1,4096]{1,0:T(1,128)} %bitcast.2, bf16[32,4096]{1,0:T(8,128)(2,1)} %dec_hbm.1, f32[1,4096]{1,0:T(1,128)} %bitcast.3, ...), custom_call_target="tpu_custom_call" | custom-call | tf_op jit(solution)/shard_map/cross_attention/pallas_call | solution.py:505
  134.2 1.0 copy.14
  135.2 0.7 copy.15
